TPU v7x, 32 devices: a whole 2x2x4 slice. The times are simulated.
32 devices in a mesh: band: 8 (over z, y), feat: 4 (over x, core).
Axes of the slice: x: 2, y: 2, z: 4, core: 2. Of those that a mesh axis runs over, the one named last changes fastest.
Arguments:
- grid_latent: bfloat16 [16384, 512], P('band', 'feat'), may hold values from -6 to 6
- mesh_latent: bfloat16 [1280, 512], P('band', 'feat'), may hold values from -6 to 6
- edge_latent: bfloat16 [8, 4, 2048, 512], P('band', 'feat'), may hold values from -6 to 6
- edge_src: int32 [8, 8192], P('band'), may hold values from 0 to 2047
- edge_dst: int32 [8, 4, 2048], P('band', 'feat'), may hold values from 0 to 160, as said below
- edge_w1: bfloat16 [1536, 512], replicated, may hold values from -0.15625 to 0.15625
- edge_b1: float32 [512], replicated, may hold values from -3 to 3
- edge_w2: bfloat16 [512, 512], replicated, may hold values from -0.25 to 0.25
- edge_b2: float32 [512], replicated, may hold values from -2 to 2
- edge_gain: float32 [512], replicated, may hold values from 0.25 to 1.75
- edge_shift: float32 [512], replicated, may hold values from -2 to 2
- node_w1: bfloat16 [1024, 512], replicated, may hold values from -0.1875 to 0.1875
- node_b1: float32 [512], replicated, may hold values from -3 to 3
- node_w2: bfloat16 [512, 512], replicated, may hold values from -0.25 to 0.25
- node_b2: float32 [512], replicated, may hold values from -2 to 2
- node_gain: float32 [512], replicated, may hold values from 0.25 to 1.75
- node_shift: float32 [512], replicated, may hold values from -2 to 2
Outputs:
- mesh_new: bfloat16 [1280, 512], P('band', 'feat')
Inputs may be any that keep to these rules, and one draw needn't show every extreme that they name: `edge_src`: entry [s, d * 1024 + j] is the grid row, counted within band index s, that sends slot j of the edges from band index s to band index d; empty slots hold some row too. `edge_dst`: entry [d, f, s * 256 + q] is the mesh node, counted within band index d, that receives slot f * 256 + q of the edges from band index s to band index d, or 160 where that slot is empty. The used slots of a pair come first; a pair has at most 1024 used slots. Each receiving band index d hears only from the sending band indices of one latitude span of consecutive indices (edges are local), which lies anywhere along band since mesh partitions are face-major; other pairs are empty. In every draw some band indices receive 1024 from every band index of their span.
All inputs are finite; a program needn't handle non-finite values.
Results may differ from a plain program's by a relative error of at most 0.011.
Values may be sent and summed in bfloat16 or wider, within the bound.
A program may use at most 64 MiB of HBM per device.

v0:
```python
import math
import jax
import jax.numpy as jnp
from jax import lax
from jax.sharding import PartitionSpec as P

EPSILON = 1e-05


def normalize(values, norm_gain, norm_shift):
    average = jnp.mean(values, -1, keepdims=True)
    centered = values - average
    variance = jnp.mean(centered * centered, -1, keepdims=True)
    return centered * lax.rsqrt(variance + EPSILON) * norm_gain + norm_shift


def node_step(row_block, summed, node_w1, node_b1, node_w2, node_b2, node_gain, node_shift):
    full_width = row_block.shape[1]
    hidden = jnp.dot(row_block, node_w1[:full_width], preferred_element_type=jnp.float32)
    hidden = (
        hidden
        + jnp.dot(
            summed.astype(jnp.bfloat16), node_w1[full_width:], preferred_element_type=jnp.float32
        )
        + node_b1
    )
    active = jax.nn.silu(hidden).astype(jnp.bfloat16)
    update = jnp.dot(active, node_w2, preferred_element_type=jnp.float32) + node_b2
    return (row_block.astype(jnp.float32) + normalize(update, node_gain, node_shift)).astype(
        jnp.bfloat16
    )


def select_rows(table, indices):
    total = indices.shape[0]
    block_rows = math.gcd(total, 512)
    grouped = indices.reshape(total // block_rows, block_rows)

    def one_block(block_ids):
        row_ids = lax.broadcasted_iota(jnp.int32, (block_rows, table.shape[0]), 1)
        onehot = (row_ids == block_ids[:, None]).astype(table.dtype)
        return jnp.dot(onehot, table, preferred_element_type=jnp.float32).astype(table.dtype)

    return lax.map(one_block, grouped).reshape(total, table.shape[1])


def body(
    grid_latent,
    mesh_latent,
    edge_latent,
    edge_src,
    edge_dst,
    edge_w1,
    edge_b1,
    edge_w2,
    edge_b2,
    edge_gain,
    edge_shift,
    node_w1,
    node_b1,
    node_w2,
    node_b2,
    node_gain,
    node_shift,
):
    band_count = lax.axis_size("band")
    feat_count = lax.axis_size("feat")
    quarter = grid_latent.shape[1]
    full_width = quarter * feat_count
    mesh_count = mesh_latent.shape[0]
    picked = select_rows(grid_latent, edge_src.reshape(-1)).reshape(band_count, -1, quarter)
    regrouped = lax.all_to_all(picked, "feat", split_axis=1, concat_axis=2, tiled=True)
    arrived = lax.all_to_all(regrouped, "band", split_axis=0, concat_axis=0, tiled=True)
    senders = arrived.reshape(-1, full_width)
    own_edges = edge_latent.reshape(-1, full_width)
    targets = edge_dst.reshape(-1)
    recv_weight = edge_w1[2 * full_width :]
    portion = lax.all_gather(mesh_latent, "feat", axis=1, tiled=True)
    projected = jnp.dot(portion, recv_weight, preferred_element_type=jnp.float32)
    node_ids = lax.broadcasted_iota(jnp.int32, (mesh_count, targets.shape[0]), 0)
    clipped = jnp.minimum(targets, mesh_count - 1)
    pick_node = (node_ids == clipped[None, :]).astype(jnp.float32)
    receiver_part = lax.dot_general(
        pick_node,
        projected,
        (((0,), (0,)), ((), ())),
        precision=lax.Precision.HIGHEST,
        preferred_element_type=jnp.float32,
    )
    hidden = jnp.dot(own_edges, edge_w1[:full_width], preferred_element_type=jnp.float32)
    hidden = hidden + jnp.dot(
        senders, edge_w1[full_width : 2 * full_width], preferred_element_type=jnp.float32
    )
    hidden = hidden + receiver_part + edge_b1
    active = jax.nn.silu(hidden).astype(jnp.bfloat16)
    update = jnp.dot(active, edge_w2, preferred_element_type=jnp.float32) + edge_b2
    edge_new = (own_edges.astype(jnp.float32) + normalize(update, edge_gain, edge_shift)).astype(
        jnp.bfloat16
    )
    selector = (node_ids == targets[None, :]).astype(jnp.bfloat16)
    partial_sums = jnp.dot(selector, edge_new, preferred_element_type=jnp.float32)
    summed = lax.psum(partial_sums.astype(jnp.bfloat16), "feat").astype(jnp.float32)
    updated = node_step(portion, summed, node_w1, node_b1, node_w2, node_b2, node_gain, node_shift)
    own_cols = lax.dynamic_slice_in_dim(updated, lax.axis_index("feat") * quarter, quarter, 1)
    return own_cols


def solution(mesh):
    placed = (
        P("band", "feat"),
        P("band", "feat"),
        P("band", "feat", None, None),
        P("band", None),
        P("band", "feat", None),
        P(),
        P(),
        P(),
        P(),
        P(),
        P(),
        P(),
        P(),
        P(),
        P(),
        P(),
        P(),
    )
    return jax.shard_map(
        body, mesh=mesh, in_specs=placed, out_specs=P("band", "feat"), check_vma=False
    )
```

profile of v0, /device:TPU:0, one launch (start us, length us, event | category | flops | bytes accessed | tf_op | source)
XLA Modules:
  0.0 183.7 jit_solution(7006882849579234291)
XLA Ops:
  7.0 1.4 reduce.3
  8.5 31.7 %while.10 = (s32[]{:T(128)}, bf16[16,512,128]{2,1,0:T(8,128)(2,1)S(1)}, s32[16,512]{1,0:T(8,128)S(1)}, bf16[2048,128]{1,0:T(8,128)(2,1)}, s32[]{:T(128)}) while((s32[]{:T(128)}, bf16[16,512,128]{2,1,0:T(8,128)(2,1)S(1)}, s32[16,512]{1,0:T(8,128)S(1)}, bf16[2048,128]{1,0:T(8,128)(2,1)}, s32[]{:T(128)}) %tuple.21), condition=%wide.region_1.2_spmd, body=%wide.region_0.1_spmd.sunk | while | flops 269549568 | bytes 661573 | solution.py:44
  8.5 1.9 %fusion.46 = bf16[16,512,128]{2,1,0:T(8,128)(2,1)S(1)} fusion(bf16[16,512,128]{2,1,0:T(8,128)(2,1)S(1)} %get-tuple-element.73, s32[]{:T(128)} %get-tuple-element.72, bf16[2048,128]{1,0:T(8,128)(2,1)} %get-tuple-element.80, s32[512]{0:T(512)S(1)} %bitcast.39), kind=kOutput, calls=%fused_computation.5.clone.1 | convolution fusion | flops 269549568 | bytes 657412 | tf_op jit(solution)/shard_map/while/body/eval_jaxpr/dot_general | solution.py:42
  10.5 1.9 %fusion.46 = bf16[16,512,128]{2,1,0:T(8,128)(2,1)S(1)} fusion(bf16[16,512,128]{2,1,0:T(8,128)(2,1)S(1)} %get-tuple-element.73, s32[]{:T(128)} %get-tuple-element.72, bf16[2048,128]{1,0:T(8,128)(2,1)} %get-tuple-element.80, s32[512]{0:T(512)S(1)} %bitcast.39), kind=kOutput, calls=%fused_computation.5.clone.1 | convolution fusion | flops 269549568 | bytes 657412 | tf_op jit(solution)/shard_map/while/body/eval_jaxpr/dot_general | solution.py:42
  12.4 1.9 %fusion.46 = bf16[16,512,128]{2,1,0:T(8,128)(2,1)S(1)} fusion(bf16[16,512,128]{2,1,0:T(8,128)(2,1)S(1)} %get-tuple-element.73, s32[]{:T(128)} %get-tuple-element.72, bf16[2048,128]{1,0:T(8,128)(2,1)} %get-tuple-element.80, s32[512]{0:T(512)S(1)} %bitcast.39), kind=kOutput, calls=%fused_computation.5.clone.1 | convolution fusion | flops 269549568 | bytes 657412 | tf_op jit(solution)/shard_map/while/body/eval_jaxpr/dot_general | solution.py:42
  14.4 1.9 %fusion.46 = bf16[16,512,128]{2,1,0:T(8,128)(2,1)S(1)} fusion(bf16[16,512,128]{2,1,0:T(8,128)(2,1)S(1)} %get-tuple-element.73, s32[]{:T(128)} %get-tuple-element.72, bf16[2048,128]{1,0:T(8,128)(2,1)} %get-tuple-element.80, s32[512]{0:T(512)S(1)} %bitcast.39), kind=kOutput, calls=%fused_computation.5.clone.1 | convolution fusion | flops 269549568 | bytes 657412 | tf_op jit(solution)/shard_map/while/body/eval_jaxpr/dot_general | solution.py:42
  16.4 1.9 %fusion.46 = bf16[16,512,128]{2,1,0:T(8,128)(2,1)S(1)} fusion(bf16[16,512,128]{2,1,0:T(8,128)(2,1)S(1)} %get-tuple-element.73, s32[]{:T(128)} %get-tuple-element.72, bf16[2048,128]{1,0:T(8,128)(2,1)} %get-tuple-element.80, s32[512]{0:T(512)S(1)} %bitcast.39), kind=kOutput, calls=%fused_computation.5.clone.1 | convolution fusion | flops 269549568 | bytes 657412 | tf_op jit(solution)/shard_map/while/body/eval_jaxpr/dot_general | solution.py:42
  18.4 1.9 %fusion.46 = bf16[16,512,128]{2,1,0:T(8,128)(2,1)S(1)} fusion(bf16[16,512,128]{2,1,0:T(8,128)(2,1)S(1)} %get-tuple-element.73, s32[]{:T(128)} %get-tuple-element.72, bf16[2048,128]{1,0:T(8,128)(2,1)} %get-tuple-element.80, s32[512]{0:T(512)S(1)} %bitcast.39), kind=kOutput, calls=%fused_computation.5.clone.1 | convolution fusion | flops 269549568 | bytes 657412 | tf_op jit(solution)/shard_map/while/body/eval_jaxpr/dot_general | solution.py:42
  20.4 1.9 %fusion.46 = bf16[16,512,128]{2,1,0:T(8,128)(2,1)S(1)} fusion(bf16[16,512,128]{2,1,0:T(8,128)(2,1)S(1)} %get-tuple-element.73, s32[]{:T(128)} %get-tuple-element.72, bf16[2048,128]{1,0:T(8,128)(2,1)} %get-tuple-element.80, s32[512]{0:T(512)S(1)} %bitcast.39), kind=kOutput, calls=%fused_computation.5.clone.1 | convolution fusion | flops 269549568 | bytes 657412 | tf_op jit(solution)/shard_map/while/body/eval_jaxpr/dot_general | solution.py:42
  22.3 1.9 %fusion.46 = bf16[16,512,128]{2,1,0:T(8,128)(2,1)S(1)} fusion(bf16[16,512,128]{2,1,0:T(8,128)(2,1)S(1)} %get-tuple-element.73, s32[]{:T(128)} %get-tuple-element.72, bf16[2048,128]{1,0:T(8,128)(2,1)} %get-tuple-element.80, s32[512]{0:T(512)S(1)} %bitcast.39), kind=kOutput, calls=%fused_computation.5.clone.1 | convolution fusion | flops 269549568 | bytes 657412 | tf_op jit(solution)/shard_map/while/body/eval_jaxpr/dot_general | solution.py:42
  24.3 1.9 %fusion.46 = bf16[16,512,128]{2,1,0:T(8,128)(2,1)S(1)} fusion(bf16[16,512,128]{2,1,0:T(8,128)(2,1)S(1)} %get-tuple-element.73, s32[]{:T(128)} %get-tuple-element.72, bf16[2048,128]{1,0:T(8,128)(2,1)} %get-tuple-element.80, s32[512]{0:T(512)S(1)} %bitcast.39), kind=kOutput, calls=%fused_computation.5.clone.1 | convolution fusion | flops 269549568 | bytes 657412 | tf_op jit(solution)/shard_map/while/body/eval_jaxpr/dot_general | solution.py:42
  26.3 1.9 %fusion.46 = bf16[16,512,128]{2,1,0:T(8,128)(2,1)S(1)} fusion(bf16[16,512,128]{2,1,0:T(8,128)(2,1)S(1)} %get-tuple-element.73, s32[]{:T(128)} %get-tuple-element.72, bf16[2048,128]{1,0:T(8,128)(2,1)} %get-tuple-element.80, s32[512]{0:T(512)S(1)} %bitcast.39), kind=kOutput, calls=%fused_computation.5.clone.1 | convolution fusion | flops 269549568 | bytes 657412 | tf_op jit(solution)/shard_map/while/body/eval_jaxpr/dot_general | solution.py:42
  28.3 1.9 %fusion.46 = bf16[16,512,128]{2,1,0:T(8,128)(2,1)S(1)} fusion(bf16[16,512,128]{2,1,0:T(8,128)(2,1)S(1)} %get-tuple-element.73, s32[]{:T(128)} %get-tuple-element.72, bf16[2048,128]{1,0:T(8,128)(2,1)} %get-tuple-element.80, s32[512]{0:T(512)S(1)} %bitcast.39), kind=kOutput, calls=%fused_computation.5.clone.1 | convolution fusion | flops 269549568 | bytes 657412 | tf_op jit(solution)/shard_map/while/body/eval_jaxpr/dot_general | solution.py:42
  30.3 1.9 %fusion.46 = bf16[16,512,128]{2,1,0:T(8,128)(2,1)S(1)} fusion(bf16[16,512,128]{2,1,0:T(8,128)(2,1)S(1)} %get-tuple-element.73, s32[]{:T(128)} %get-tuple-element.72, bf16[2048,128]{1,0:T(8,128)(2,1)} %get-tuple-element.80, s32[512]{0:T(512)S(1)} %bitcast.39), kind=kOutput, calls=%fused_computation.5.clone.1 | convolution fusion | flops 269549568 | bytes 657412 | tf_op jit(solution)/shard_map/while/body/eval_jaxpr/dot_general | solution.py:42
  32.2 1.9 %fusion.46 = bf16[16,512,128]{2,1,0:T(8,128)(2,1)S(1)} fusion(bf16[16,512,128]{2,1,0:T(8,128)(2,1)S(1)} %get-tuple-element.73, s32[]{:T(128)} %get-tuple-element.72, bf16[2048,128]{1,0:T(8,128)(2,1)} %get-tuple-element.80, s32[512]{0:T(512)S(1)} %bitcast.39), kind=kOutput, calls=%fused_computation.5.clone.1 | convolution fusion | flops 269549568 | bytes 657412 | tf_op jit(solution)/shard_map/while/body/eval_jaxpr/dot_general | solution.py:42
  34.2 1.9 %fusion.46 = bf16[16,512,128]{2,1,0:T(8,128)(2,1)S(1)} fusion(bf16[16,512,128]{2,1,0:T(8,128)(2,1)S(1)} %get-tuple-element.73, s32[]{:T(128)} %get-tuple-element.72, bf16[2048,128]{1,0:T(8,128)(2,1)} %get-tuple-element.80, s32[512]{0:T(512)S(1)} %bitcast.39), kind=kOutput, calls=%fused_computation.5.clone.1 | convolution fusion | flops 269549568 | bytes 657412 | tf_op jit(solution)/shard_map/while/body/eval_jaxpr/dot_general | solution.py:42
  36.2 1.9 %fusion.46 = bf16[16,512,128]{2,1,0:T(8,128)(2,1)S(1)} fusion(bf16[16,512,128]{2,1,0:T(8,128)(2,1)S(1)} %get-tuple-element.73, s32[]{:T(128)} %get-tuple-element.72, bf16[2048,128]{1,0:T(8,128)(2,1)} %get-tuple-element.80, s32[512]{0:T(512)S(1)} %bitcast.39), kind=kOutput, calls=%fused_computation.5.clone.1 | convolution fusion | flops 269549568 | bytes 657412 | tf_op jit(solution)/shard_map/while/body/eval_jaxpr/dot_general | solution.py:42
  38.2 1.9 %fusion.46 = bf16[16,512,128]{2,1,0:T(8,128)(2,1)S(1)} fusion(bf16[16,512,128]{2,1,0:T(8,128)(2,1)S(1)} %get-tuple-element.73, s32[]{:T(128)} %get-tuple-element.72, bf16[2048,128]{1,0:T(8,128)(2,1)} %get-tuple-element.80, s32[512]{0:T(512)S(1)} %bitcast.39), kind=kOutput, calls=%fused_computation.5.clone.1 | convolution fusion | flops 269549568 | bytes 657412 | tf_op jit(solution)/shard_map/while/body/eval_jaxpr/dot_general | solution.py:42
  41.5 29.8 %all_to_all.23 = bf16[8,1024,128]{2,0,1:T(8,128)(2,1)} all-to-all(bf16[8,1024,128]{2,0,1:T(8,128)(2,1)S(1)} %copy.28), channel_id=1, replica_groups=mesh['band'=8,'feat'=4] {'feat'}, dimensions={1} | all-to-all | bytes 4194304 | tf_op jit(solution)/shard_map/all_to_all | solution.py:72
  71.3 4.5 %copy.30 = bf16[8,256,4,128]{1,3,2,0:T(8,128)(2,1)} copy(bf16[8,256,4,128]{3,0,1,2:T(8,128)(2,1)} %bitcast.37) | data formatting | bytes 4194304 | tf_op jit(solution)/shard_map/all_to_all | solution.py:72
  75.8 6.5 %all-to-all-start.1 = ((bf16[8,256,512]{1,2,0:T(8,128)(2,1)}), bf16[8,256,512]{1,2,0:T(8,128)(2,1)}, u32[]{:S(2)}, u32[]{:S(2)}) async-start(bf16[8,256,512]{1,2,0:T(8,128)(2,1)} %bitcast.36), calls=%async_computation.1 | async-start | bytes 4194304 | tf_op jit(solution)/shard_map/all_to_all | solution.py:73
  82.3 2.5 %copy.27 = bf16[1,1,2048,512]{2,3,1,0:T(8,128)(2,1)} copy(bf16[1,1,2048,512]{3,2,1,0:T(8,128)(2,1)S(1)} %copy-done.1) | data formatting | bytes 4194304 | tf_op args[2]
  84.8 5.7 %all_gather.3 = bf16[160,512]{1,0:T(8,128)(2,1)S(1)} all-gather(bf16[160,128]{1,0:T(8,128)(2,1)S(1)} %copy-done.5), channel_id=1, replica_groups=mesh['band'=8,'feat'=4] {'feat'}, dimensions={1}, use_global_device_ids=true | all-gather | bytes 204800 | tf_op jit(solution)/shard_map/all_gather | solution.py:78
  91.8 4.2 %fusion.5 = f32[2048,512]{1,0:T(8,128)} fusion(bf16[1,1,2048,512]{3,2,1,0:T(8,128)(2,1)S(1)} %copy-done.1, bf16[1536,512]{1,0:T(8,128)(2,1)} %param.24), kind=kOutput, calls=%fused_computation.11 | convolution fusion | flops 1073741824 | bytes 6815744 | tf_op jit(solution)/shard_map/dot_general | solution.py:90
  96.1 34.2 %all-to-all-done.1 = bf16[8,256,512]{1,2,0:T(8,128)(2,1)} async-done(((bf16[8,256,512]{1,2,0:T(8,128)(2,1)}), bf16[8,256,512]{1,2,0:T(8,128)(2,1)}, u32[]{:S(2)}, u32[]{:S(2)}) %all-to-all-start.1) | async-done | bytes 2097184 | tf_op jit(solution)/shard_map/all_to_all | solution.py:73
  130.3 2.9 %copy.31 = bf16[8,256,512]{2,1,0:T(8,128)(2,1)S(1)} copy(bf16[8,256,512]{1,2,0:T(8,128)(2,1)} %all-to-all-done.1) | data formatting | bytes 4194304 | tf_op jit(solution)/shard_map/all_to_all | solution.py:73
  133.2 2.4 %fusion.15 = f32[2048,512]{1,0:T(8,128)S(1)} fusion(bf16[2048,512]{1,0:T(8,128)(2,1)S(1)} %bitcast.35, bf16[1536,512]{1,0:T(8,128)(2,1)} %param.24), kind=kOutput, calls=%fused_computation.25 | convolution fusion | flops 1073741824 | bytes 6815744 | tf_op jit(solution)/shard_map/dot_general | solution.py:91
  135.6 3.0 %multiply_convert_fusion = bf16[2048,512]{1,0:T(8,128)(2,1)S(1)} fusion(f32[2048,512]{1,0:T(8,128)S(1)} %copy-done.2, f32[2048,512]{1,0:T(8,128)S(1)} %fusion.15, f32[160,512]{1,0:T(8,128)S(1)} %fusion.13, f32[512]{0:T(512)S(1)} %copy-done.9, s32[2048]{0:T(1024)S(1)} %broadcast_minimum_fusion), kind=kOutput, calls=%fused_computation.9 | convolution fusion | flops 2021982208 | bytes 10823680 | tf_op jit(solution)/shard_map/dot_general | solution.py:83
  138.7 1.4 add_reduce_fusion
  141.7 2.3 %fusion.9 = bf16[160,512]{1,0:T(8,128)(2,1)} fusion(f32[2048,512]{0,1:T(8,128)S(1)} %get-tuple-element.39, bf16[1,1,2048,512]{2,3,1,0:T(8,128)(2,1)S(1)} %copy-done.3, f32[512]{0:T(512)S(1)} %copy-done.10, f32[512]{0:T(512)S(1)} %copy-done.11, f32[2048]{0:T(1024)S(1)} %add_rsqrt_fusion, f32[2048]{0:T(1024)S(1)} %broadcast_multiply_fusion, ...), kind=kOutput, calls=%fused_computation.19 | convolution fusion | flops 344342528 | bytes 6486016 | tf_op jit(solution)/shard_map/dot_general | solution.py:101
  145.7 28.6 %all-reduce.2.cloned.1.call-done = bf16[160,512]{1,0:T(8,128)(2,1)} async-done(((bf16[160,512]{1,0:T(8,128)(2,1)}), bf16[160,512]{1,0:T(8,128)(2,1)}) %all-reduce.2.cloned.1.call-update) | async-done | bytes 163856 | tf_op jit(solution)/shard_map/psum | solution.py:102
  174.4 1.5 fusion.31
  (62 shorter events, 7.7 us)
Async XLA Ops:
  6.5 132.1 %copy-start = (bf16[512,512]{1,0:T(8,128)(2,1)S(1)}, bf16[512,512]{1,0:T(8,128)(2,1)}, u32[]{:S(2)}) copy-start(bf16[512,512]{1,0:T(8,128)(2,1)} %param.26) | copy-start | bytes 1572868
  71.3 11.0 %copy-start.1 = (bf16[1,1,2048,512]{3,2,1,0:T(8,128)(2,1)S(1)}, bf16[1,1,2048,512]{3,2,1,0:T(8,128)(2,1)}, u32[]{:S(2)}) copy-start(bf16[1,1,2048,512]{3,2,1,0:T(8,128)(2,1)} %param.21) | copy-start | bytes 6291460
  75.8 9.1 %copy-start.5 = (bf16[160,128]{1,0:T(8,128)(2,1)S(1)}, bf16[160,128]{1,0:T(8,128)(2,1)}, u32[]{:S(2)}) copy-start(bf16[160,128]{1,0:T(8,128)(2,1)} %param.20) | copy-start | bytes 122884
  75.8 14.8 %copy-start.6 = (s32[1,1,2048]{2,1,0:T(1,128)S(1)}, s32[1,1,2048]{2,1,0:T(1,128)}, u32[]{:S(2)}) copy-start(s32[1,1,2048]{2,1,0:T(1,128)} %param.23) | copy-start | bytes 24580
  75.8 54.5 %all-to-all-start.1 = ((bf16[8,256,512]{1,2,0:T(8,128)(2,1)}), bf16[8,256,512]{1,2,0:T(8,128)(2,1)}, u32[]{:S(2)}, u32[]{:S(2)}) async-start(bf16[8,256,512]{1,2,0:T(8,128)(2,1)} %bitcast.36), calls=%async_computation.1 | async-start | bytes 4194304 | tf_op jit(solution)/shard_map/all_to_all | solution.py:73
  82.3 92.1 %all-reduce.2.cloned.1.call-start = ((), (), s32[]{:S(2)}) async-start(), calls=%async_computation.2 | async-start | bytes 327680 | tf_op jit(solution)/shard_map/psum | solution.py:102
  133.1 2.5 %copy-start.2 = (f32[2048,512]{1,0:T(8,128)S(1)}, f32[2048,512]{1,0:T(8,128)}, u32[]{:S(2)}) copy-start(f32[2048,512]{1,0:T(8,128)} %fusion.5) | copy-start | bytes 12582916
  133.1 2.5 %copy-start.9 = (f32[512]{0:T(512)S(1)}, f32[512]{0:T(512)}, u32[]{:S(2)}) copy-start(f32[512]{0:T(512)} %param.25) | copy-start | bytes 6148
  135.6 3.0 %copy-start.7 = (f32[512]{0:T(512)S(1)}, f32[512]{0:T(512)}, u32[]{:S(2)}) copy-start(f32[512]{0:T(512)} %param.27) | copy-start | bytes 6148
  140.0 1.6 copy-start.3
  140.1 1.6 copy-start.10
  140.1 1.6 copy-start.11
  141.6 2.3 %copy-start.4 = (bf16[1024,512]{1,0:T(8,128)(2,1)S(1)}, bf16[1024,512]{1,0:T(8,128)(2,1)}, u32[]{:S(2)}) copy-start(bf16[1024,512]{1,0:T(8,128)(2,1)} %param.30) | copy-start | bytes 3145732
  141.6 32.7 %copy-start.8 = (bf16[512,512]{1,0:T(8,128)(2,1)S(1)}, bf16[512,512]{1,0:T(8,128)(2,1)}, u32[]{:S(2)}) copy-start(bf16[512,512]{1,0:T(8,128)(2,1)} %param.32) | copy-start | bytes 1572868
  141.6 32.7 %copy-start.12 = (f32[512]{0:T(512)S(1)}, f32[512]{0:T(512)}, u32[]{:S(2)}) copy-start(f32[512]{0:T(512)} %param.33) | copy-start | bytes 6148
  141.7 32.7 %copy-start.13 = (f32[512]{0:T(512)S(1)}, f32[512]{0:T(512)}, u32[]{:S(2)}) copy-start(f32[512]{0:T(512)} %param.31) | copy-start | bytes 6148
Sparse Core Ops, SparseCore 0:
  144.1 30.2 all-reduce.1
where the time goes:
time: 185 us; the launch traced here: 184 us
  waiting for transfers between devices  62.9 us (34%)
  matrix products  47.5 us (26%)
  blocking collectives  35.5 us (19%)
  local copies, waits for them, and re-layouts  14.3 us (8%)
  between operations  13.6 us (7%)
  starting transfers between devices  6.57 us (4%)
  other arithmetic  2.98 us (2%)
    all_to_all x1, waiting for transfers between devices, body(): lax.all_to_all(regrouped, 'band', split_axis=0, concat_axis=0, tiled=True)  34.2 us
    dot_general x16, matrix products, one_block(): jnp.dot(onehot, table, preferred_element_type=jnp.float32)  31.1 us
    all_to_all x1, blocking collectives, body(): lax.all_to_all(picked, 'feat', split_axis=1, concat_axis=2, tiled=True)  29.8 us
    psum x1, waiting for transfers between devices, body(): lax.psum(partial_sums.astype(jnp.bfloat16), 'feat').astype(jnp.float32)  28.6 us
    all_to_all x1, starting transfers between devices, body(): lax.all_to_all(regrouped, 'band', split_axis=0, concat_axis=0, tiled=True)  6.53 us
    all_gather x1, blocking collectives, body(): portion = lax.all_gather(mesh_latent, 'feat', axis=1, tiled=True)  5.7 us
    all_to_all x1, local copies, waits for them, and re-layouts, body(): lax.all_to_all(picked, 'feat', split_axis=1, concat_axis=2, tiled=True)  4.46 us
    dot_general x1, matrix products, body(): jnp.dot(own_edges, edge_w1[:full_width], preferred_element_type=jnp.float32)  4.22 us
  transfers between devices with their start and end apart: 2, of which 2 were waited for; matrix products, arithmetic and copies ran while one was open for 5% of the time, Pallas kernels for 0%

commit v1 on v0

--- a/solution.py
+++ b/solution.py
@@ -99,7 +99,9 @@
     )
     selector = (node_ids == targets[None, :]).astype(jnp.bfloat16)
     partial_sums = jnp.dot(selector, edge_new, preferred_element_type=jnp.float32)
-    summed = lax.psum(partial_sums.astype(jnp.bfloat16), "feat").astype(jnp.float32)
+    summed = jnp.sum(lax.all_gather(partial_sums.astype(jnp.bfloat16), "feat"), axis=0).astype(
+        jnp.float32
+    )
     updated = node_step(portion, summed, node_w1, node_b1, node_w2, node_b2, node_gain, node_shift)
     own_cols = lax.dynamic_slice_in_dim(updated, lax.axis_index("feat") * quarter, quarter, 1)
     return own_cols

time: 185 us -> 148 us (0.80)
  waiting for transfers between devices: 62.9 us -> 31.5 us
  between operations: 13.6 us -> 0.22 us
  blocking collectives: 35.5 us -> 42.7 us
    psum x1 -> x0, waiting for transfers between devices: 28.6 us -> none  [body(): lax.psum(partial_sums.astype(jnp.bfloat16), 'feat').astype(jnp.float32)]
    all_gather x0 -> x1, blocking collectives: none -> 7.19 us  [body(): lax.all_gather(partial_sums.astype(jnp.bfloat16), 'feat')]
    all_to_all x1, waiting for transfers between devices: 34.2 us -> 31.5 us  [body(): lax.all_to_all(regrouped, 'band', split_axis=0, concat_axis=0, tiled=True)]
    unnamed x30 -> x26, local copies, waits for them, and re-layouts: 3.95 us -> 3.92 us
  transfers between devices with their start and end apart: 2 -> 1, of which waited for: 2 -> 1; matrix products, arithmetic and copies ran while one was open for 5% -> 7% of each run, Pallas kernels for 0% -> 0%
where the time goes in v1:
time: 148 us; the launch traced here: 147 us
  matrix products  48.1 us (32%)
  blocking collectives  42.7 us (29%)
  waiting for transfers between devices  31.5 us (21%)
  local copies, waits for them, and re-layouts  14.3 us (10%)
  starting transfers between devices  6.53 us (4%)
  other arithmetic  3.07 us (2%)
    all_to_all x1, waiting for transfers between devices, body(): lax.all_to_all(regrouped, 'band', split_axis=0, concat_axis=0, tiled=True)  31.5 us
    dot_general x16, matrix products, one_block(): jnp.dot(onehot, table, preferred_element_type=jnp.float32)  31.1 us
    all_to_all x1, blocking collectives, body(): lax.all_to_all(picked, 'feat', split_axis=1, concat_axis=2, tiled=True)  29.8 us
    all_gather x1, blocking collectives, body(): lax.all_gather(partial_sums.astype(jnp.bfloat16), 'feat')  7.19 us
    all_to_all x1, starting transfers between devices, body(): lax.all_to_all(regrouped, 'band', split_axis=0, concat_axis=0, tiled=True)  6.53 us
    all_gather x1, blocking collectives, body(): portion = lax.all_gather(mesh_latent, 'feat', axis=1, tiled=True)  5.7 us
    all_to_all x1, local copies, waits for them, and re-layouts, body(): lax.all_to_all(picked, 'feat', split_axis=1, concat_axis=2, tiled=True)  4.51 us
    dot_general x1, matrix products, body(): jnp.dot(own_edges, edge_w1[:full_width], preferred_element_type=jnp.float32)  4.23 us
  transfers between devices with their start and end apart: 1, of which 1 were waited for; matrix products, arithmetic and copies ran while one was open for 7% of the time, Pallas kernels for 0%

profile of v1, /device:TPU:0, one launch (start us, length us, event | category | flops | bytes accessed | tf_op | source)
XLA Modules:
  0.0 146.8 jit_solution(8575531765120464572)
XLA Ops:
  0.5 1.4 reduce.4
  1.9 31.7 %while.10 = (s32[]{:T(128)}, bf16[16,512,128]{2,1,0:T(8,128)(2,1)S(1)}, s32[16,512]{1,0:T(8,128)S(1)}, bf16[2048,128]{1,0:T(8,128)(2,1)}, s32[]{:T(128)}) while((s32[]{:T(128)}, bf16[16,512,128]{2,1,0:T(8,128)(2,1)S(1)}, s32[16,512]{1,0:T(8,128)S(1)}, bf16[2048,128]{1,0:T(8,128)(2,1)}, s32[]{:T(128)}) %tuple.21), condition=%wide.region_1.2_spmd, body=%wide.region_0.1_spmd.sunk | while | flops 269549568 | bytes 661573 | solution.py:44
  1.9 1.9 %fusion.46 = bf16[16,512,128]{2,1,0:T(8,128)(2,1)S(1)} fusion(bf16[16,512,128]{2,1,0:T(8,128)(2,1)S(1)} %get-tuple-element.73, s32[]{:T(128)} %get-tuple-element.72, bf16[2048,128]{1,0:T(8,128)(2,1)} %get-tuple-element.80, s32[512]{0:T(512)S(1)} %bitcast.41), kind=kOutput, calls=%fused_computation.5.clone.1 | convolution fusion | flops 269549568 | bytes 657412 | tf_op jit(solution)/shard_map/while/body/eval_jaxpr/dot_general | solution.py:42
  3.9 1.9 %fusion.46 = bf16[16,512,128]{2,1,0:T(8,128)(2,1)S(1)} fusion(bf16[16,512,128]{2,1,0:T(8,128)(2,1)S(1)} %get-tuple-element.73, s32[]{:T(128)} %get-tuple-element.72, bf16[2048,128]{1,0:T(8,128)(2,1)} %get-tuple-element.80, s32[512]{0:T(512)S(1)} %bitcast.41), kind=kOutput, calls=%fused_computation.5.clone.1 | convolution fusion | flops 269549568 | bytes 657412 | tf_op jit(solution)/shard_map/while/body/eval_jaxpr/dot_general | solution.py:42
  5.9 1.9 %fusion.46 = bf16[16,512,128]{2,1,0:T(8,128)(2,1)S(1)} fusion(bf16[16,512,128]{2,1,0:T(8,128)(2,1)S(1)} %get-tuple-element.73, s32[]{:T(128)} %get-tuple-element.72, bf16[2048,128]{1,0:T(8,128)(2,1)} %get-tuple-element.80, s32[512]{0:T(512)S(1)} %bitcast.41), kind=kOutput, calls=%fused_computation.5.clone.1 | convolution fusion | flops 269549568 | bytes 657412 | tf_op jit(solution)/shard_map/while/body/eval_jaxpr/dot_general | solution.py:42
  7.9 1.9 %fusion.46 = bf16[16,512,128]{2,1,0:T(8,128)(2,1)S(1)} fusion(bf16[16,512,128]{2,1,0:T(8,128)(2,1)S(1)} %get-tuple-element.73, s32[]{:T(128)} %get-tuple-element.72, bf16[2048,128]{1,0:T(8,128)(2,1)} %get-tuple-element.80, s32[512]{0:T(512)S(1)} %bitcast.41), kind=kOutput, calls=%fused_computation.5.clone.1 | convolution fusion | flops 269549568 | bytes 657412 | tf_op jit(solution)/shard_map/while/body/eval_jaxpr/dot_general | solution.py:42
  9.9 1.9 %fusion.46 = bf16[16,512,128]{2,1,0:T(8,128)(2,1)S(1)} fusion(bf16[16,512,128]{2,1,0:T(8,128)(2,1)S(1)} %get-tuple-element.73, s32[]{:T(128)} %get-tuple-element.72, bf16[2048,128]{1,0:T(8,128)(2,1)} %get-tuple-element.80, s32[512]{0:T(512)S(1)} %bitcast.41), kind=kOutput, calls=%fused_computation.5.clone.1 | convolution fusion | flops 269549568 | bytes 657412 | tf_op jit(solution)/shard_map/while/body/eval_jaxpr/dot_general | solution.py:42
  11.8 1.9 %fusion.46 = bf16[16,512,128]{2,1,0:T(8,128)(2,1)S(1)} fusion(bf16[16,512,128]{2,1,0:T(8,128)(2,1)S(1)} %get-tuple-element.73, s32[]{:T(128)} %get-tuple-element.72, bf16[2048,128]{1,0:T(8,128)(2,1)} %get-tuple-element.80, s32[512]{0:T(512)S(1)} %bitcast.41), kind=kOutput, calls=%fused_computation.5.clone.1 | convolution fusion | flops 269549568 | bytes 657412 | tf_op jit(solution)/shard_map/while/body/eval_jaxpr/dot_general | solution.py:42
  13.8 1.9 %fusion.46 = bf16[16,512,128]{2,1,0:T(8,128)(2,1)S(1)} fusion(bf16[16,512,128]{2,1,0:T(8,128)(2,1)S(1)} %get-tuple-element.73, s32[]{:T(128)} %get-tuple-element.72, bf16[2048,128]{1,0:T(8,128)(2,1)} %get-tuple-element.80, s32[512]{0:T(512)S(1)} %bitcast.41), kind=kOutput, calls=%fused_computation.5.clone.1 | convolution fusion | flops 269549568 | bytes 657412 | tf_op jit(solution)/shard_map/while/body/eval_jaxpr/dot_general | solution.py:42
  15.8 1.9 %fusion.46 = bf16[16,512,128]{2,1,0:T(8,128)(2,1)S(1)} fusion(bf16[16,512,128]{2,1,0:T(8,128)(2,1)S(1)} %get-tuple-element.73, s32[]{:T(128)} %get-tuple-element.72, bf16[2048,128]{1,0:T(8,128)(2,1)} %get-tuple-element.80, s32[512]{0:T(512)S(1)} %bitcast.41), kind=kOutput, calls=%fused_computation.5.clone.1 | convolution fusion | flops 269549568 | bytes 657412 | tf_op jit(solution)/shard_map/while/body/eval_jaxpr/dot_general | solution.py:42
  17.8 1.9 %fusion.46 = bf16[16,512,128]{2,1,0:T(8,128)(2,1)S(1)} fusion(bf16[16,512,128]{2,1,0:T(8,128)(2,1)S(1)} %get-tuple-element.73, s32[]{:T(128)} %get-tuple-element.72, bf16[2048,128]{1,0:T(8,128)(2,1)} %get-tuple-element.80, s32[512]{0:T(512)S(1)} %bitcast.41), kind=kOutput, calls=%fused_computation.5.clone.1 | convolution fusion | flops 269549568 | bytes 657412 | tf_op jit(solution)/shard_map/while/body/eval_jaxpr/dot_general | solution.py:42
  19.8 1.9 %fusion.46 = bf16[16,512,128]{2,1,0:T(8,128)(2,1)S(1)} fusion(bf16[16,512,128]{2,1,0:T(8,128)(2,1)S(1)} %get-tuple-element.73, s32[]{:T(128)} %get-tuple-element.72, bf16[2048,128]{1,0:T(8,128)(2,1)} %get-tuple-element.80, s32[512]{0:T(512)S(1)} %bitcast.41), kind=kOutput, calls=%fused_computation.5.clone.1 | convolution fusion | flops 269549568 | bytes 657412 | tf_op jit(solution)/shard_map/while/body/eval_jaxpr/dot_general | solution.py:42
  21.7 1.9 %fusion.46 = bf16[16,512,128]{2,1,0:T(8,128)(2,1)S(1)} fusion(bf16[16,512,128]{2,1,0:T(8,128)(2,1)S(1)} %get-tuple-element.73, s32[]{:T(128)} %get-tuple-element.72, bf16[2048,128]{1,0:T(8,128)(2,1)} %get-tuple-element.80, s32[512]{0:T(512)S(1)} %bitcast.41), kind=kOutput, calls=%fused_computation.5.clone.1 | convolution fusion | flops 269549568 | bytes 657412 | tf_op jit(solution)/shard_map/while/body/eval_jaxpr/dot_general | solution.py:42
  23.7 1.9 %fusion.46 = bf16[16,512,128]{2,1,0:T(8,128)(2,1)S(1)} fusion(bf16[16,512,128]{2,1,0:T(8,128)(2,1)S(1)} %get-tuple-element.73, s32[]{:T(128)} %get-tuple-element.72, bf16[2048,128]{1,0:T(8,128)(2,1)} %get-tuple-element.80, s32[512]{0:T(512)S(1)} %bitcast.41), kind=kOutput, calls=%fused_computation.5.clone.1 | convolution fusion | flops 269549568 | bytes 657412 | tf_op jit(solution)/shard_map/while/body/eval_jaxpr/dot_general | solution.py:42
  25.7 1.9 %fusion.46 = bf16[16,512,128]{2,1,0:T(8,128)(2,1)S(1)} fusion(bf16[16,512,128]{2,1,0:T(8,128)(2,1)S(1)} %get-tuple-element.73, s32[]{:T(128)} %get-tuple-element.72, bf16[2048,128]{1,0:T(8,128)(2,1)} %get-tuple-element.80, s32[512]{0:T(512)S(1)} %bitcast.41), kind=kOutput, calls=%fused_computation.5.clone.1 | convolution fusion | flops 269549568 | bytes 657412 | tf_op jit(solution)/shard_map/while/body/eval_jaxpr/dot_general | solution.py:42
  27.7 1.9 %fusion.46 = bf16[16,512,128]{2,1,0:T(8,128)(2,1)S(1)} fusion(bf16[16,512,128]{2,1,0:T(8,128)(2,1)S(1)} %get-tuple-element.73, s32[]{:T(128)} %get-tuple-element.72, bf16[2048,128]{1,0:T(8,128)(2,1)} %get-tuple-element.80, s32[512]{0:T(512)S(1)} %bitcast.41), kind=kOutput, calls=%fused_computation.5.clone.1 | convolution fusion | flops 269549568 | bytes 657412 | tf_op jit(solution)/shard_map/while/body/eval_jaxpr/dot_general | solution.py:42
  29.7 1.9 %fusion.46 = bf16[16,512,128]{2,1,0:T(8,128)(2,1)S(1)} fusion(bf16[16,512,128]{2,1,0:T(8,128)(2,1)S(1)} %get-tuple-element.73, s32[]{:T(128)} %get-tuple-element.72, bf16[2048,128]{1,0:T(8,128)(2,1)} %get-tuple-element.80, s32[512]{0:T(512)S(1)} %bitcast.41), kind=kOutput, calls=%fused_computation.5.clone.1 | convolution fusion | flops 269549568 | bytes 657412 | tf_op jit(solution)/shard_map/while/body/eval_jaxpr/dot_general | solution.py:42
  31.6 1.9 %fusion.46 = bf16[16,512,128]{2,1,0:T(8,128)(2,1)S(1)} fusion(bf16[16,512,128]{2,1,0:T(8,128)(2,1)S(1)} %get-tuple-element.73, s32[]{:T(128)} %get-tuple-element.72, bf16[2048,128]{1,0:T(8,128)(2,1)} %get-tuple-element.80, s32[512]{0:T(512)S(1)} %bitcast.41), kind=kOutput, calls=%fused_computation.5.clone.1 | convolution fusion | flops 269549568 | bytes 657412 | tf_op jit(solution)/shard_map/while/body/eval_jaxpr/dot_general | solution.py:42
  35.0 29.8 %all_to_all.23 = bf16[8,1024,128]{2,0,1:T(8,128)(2,1)} all-to-all(bf16[8,1024,128]{2,0,1:T(8,128)(2,1)S(1)} %copy.28), channel_id=1, replica_groups=mesh['band'=8,'feat'=4] {'feat'}, dimensions={1} | all-to-all | bytes 4194304 | tf_op jit(solution)/shard_map/all_to_all | solution.py:72
  64.8 4.5 %copy.30 = bf16[8,256,4,128]{1,3,2,0:T(8,128)(2,1)} copy(bf16[8,256,4,128]{3,0,1,2:T(8,128)(2,1)} %bitcast.38) | data formatting | bytes 4194304 | tf_op jit(solution)/shard_map/all_to_all | solution.py:72
  69.3 6.5 %all-to-all-start.1 = ((bf16[8,256,512]{1,2,0:T(8,128)(2,1)}), bf16[8,256,512]{1,2,0:T(8,128)(2,1)}, u32[]{:S(2)}, u32[]{:S(2)}) async-start(bf16[8,256,512]{1,2,0:T(8,128)(2,1)} %bitcast.37), calls=%async_computation.1 | async-start | bytes 4194304 | tf_op jit(solution)/shard_map/all_to_all | solution.py:73
  75.8 2.5 %copy.27 = bf16[1,1,2048,512]{2,3,1,0:T(8,128)(2,1)} copy(bf16[1,1,2048,512]{3,2,1,0:T(8,128)(2,1)S(1)} %copy-done.1) | data formatting | bytes 4194304 | tf_op args[2]
  79.8 5.7 %all_gather.9 = bf16[160,512]{1,0:T(8,128)(2,1)S(1)} all-gather(bf16[160,128]{1,0:T(8,128)(2,1)S(1)} %copy-done.4), channel_id=1, replica_groups=mesh['band'=8,'feat'=4] {'feat'}, dimensions={1}, use_global_device_ids=true | all-gather | bytes 204800 | tf_op jit(solution)/shard_map/all_gather | solution.py:78
  88.1 4.2 %fusion.5 = f32[2048,512]{1,0:T(8,128)} fusion(bf16[1,1,2048,512]{3,2,1,0:T(8,128)(2,1)S(1)} %copy-done.1, bf16[1536,512]{1,0:T(8,128)(2,1)} %param.24), kind=kOutput, calls=%fused_computation.11 | convolution fusion | flops 1073741824 | bytes 6815744 | tf_op jit(solution)/shard_map/dot_general | solution.py:90
  92.3 31.5 %all-to-all-done.1 = bf16[8,256,512]{1,2,0:T(8,128)(2,1)} async-done(((bf16[8,256,512]{1,2,0:T(8,128)(2,1)}), bf16[8,256,512]{1,2,0:T(8,128)(2,1)}, u32[]{:S(2)}, u32[]{:S(2)}) %all-to-all-start.1) | async-done | bytes 2097184 | tf_op jit(solution)/shard_map/all_to_all | solution.py:73
  123.8 2.9 %copy.31 = bf16[8,256,512]{2,1,0:T(8,128)(2,1)S(1)} copy(bf16[8,256,512]{1,2,0:T(8,128)(2,1)} %all-to-all-done.1) | data formatting | bytes 4194304 | tf_op jit(solution)/shard_map/all_to_all | solution.py:73
  126.7 2.4 %fusion.15 = f32[2048,512]{1,0:T(8,128)S(1)} fusion(bf16[2048,512]{1,0:T(8,128)(2,1)S(1)} %bitcast.36, bf16[1536,512]{1,0:T(8,128)(2,1)} %param.24), kind=kOutput, calls=%fused_computation.25 | convolution fusion | flops 1073741824 | bytes 6815744 | tf_op jit(solution)/shard_map/dot_general | solution.py:91
  129.1 3.0 %multiply_convert_fusion = bf16[2048,512]{1,0:T(8,128)(2,1)S(1)} fusion(f32[2048,512]{1,0:T(8,128)S(1)} %copy-done.2, f32[2048,512]{1,0:T(8,128)S(1)} %fusion.15, f32[160,512]{1,0:T(8,128)S(1)} %fusion.13, f32[512]{0:T(512)S(1)} %copy-done.7, s32[2048]{0:T(1024)S(1)} %broadcast_minimum_fusion), kind=kOutput, calls=%fused_computation.9 | convolution fusion | flops 2021982208 | bytes 10823680 | tf_op jit(solution)/shard_map/dot_general | solution.py:83
  132.2 1.4 add_reduce_fusion
  135.2 1.6 %fusion.9 = bf16[160,512]{1,0:T(8,128)(2,1)S(1)} fusion(f32[2048,512]{0,1:T(8,128)S(1)} %get-tuple-element.39, bf16[1,1,2048,512]{2,3,1,0:T(8,128)(2,1)S(1)} %copy-done.3, f32[512]{0:T(512)S(1)} %copy-done.8, f32[512]{0:T(512)S(1)} %copy-done.9, f32[2048]{0:T(1024)S(1)} %add_rsqrt_fusion, f32[2048]{0:T(1024)S(1)} %broadcast_multiply_fusion, ...), kind=kOutput, calls=%fused_computation.19 | convolution fusion | flops 344342528 | bytes 6486016 | tf_op jit(solution)/shard_map/dot_general | solution.py:101
  136.8 7.2 %all-gather = bf16[640,512]{1,0:T(8,128)(2,1)S(1)} all-gather(bf16[160,512]{1,0:T(8,128)(2,1)S(1)} %fusion.9), channel_id=2, replica_groups=mesh['band'=8,'feat'=4] {'feat'}, dimensions={0}, use_global_device_ids=true | all-gather | bytes 819200 | tf_op jit(solution)/shard_map/all_gather | solution.py:102
  144.1 1.8 %fusion.31 = (f32[160]{0:T(256)S(1)}, f32[160,512]{1,0:T(8,128)S(1)}) fusion(f32[512]{0:T(512)S(1)} %copy-done.10, bf16[512,512]{1,0:T(8,128)(2,1)} %param.32, f32[160,512]{1,0:T(8,128)S(1)} %fusion.18, bf16[160,512]{1,0:T(8,128)(2,1)S(1)} %reduce_sum.50, bf16[1024,512]{1,0:T(8,128)(2,1)} %param.30, f32[512]{0:T(512)S(1)} %copy-done.11), kind=kOutput, calls=%fused_computation.46 | convolution fusion | flops 168509280 | bytes 1872512 | tf_op jit(solution)/shard_map/dot_general | solution.py:28
  (57 shorter events, 8.7 us)
Async XLA Ops:
  0.0 132.2 %copy-start = (bf16[512,512]{1,0:T(8,128)(2,1)S(1)}, bf16[512,512]{1,0:T(8,128)(2,1)}, u32[]{:S(2)}) copy-start(bf16[512,512]{1,0:T(8,128)(2,1)} %param.26) | copy-start | bytes 1572868
  64.8 11.0 %copy-start.1 = (bf16[1,1,2048,512]{3,2,1,0:T(8,128)(2,1)S(1)}, bf16[1,1,2048,512]{3,2,1,0:T(8,128)(2,1)}, u32[]{:S(2)}) copy-start(bf16[1,1,2048,512]{3,2,1,0:T(8,128)(2,1)} %param.21) | copy-start | bytes 6291460
  69.3 10.5 %copy-start.4 = (bf16[160,128]{1,0:T(8,128)(2,1)S(1)}, bf16[160,128]{1,0:T(8,128)(2,1)}, u32[]{:S(2)}) copy-start(bf16[160,128]{1,0:T(8,128)(2,1)} %param.20) | copy-start | bytes 122884
  69.3 16.2 %copy-start.5 = (s32[1,1,2048]{2,1,0:T(1,128)S(1)}, s32[1,1,2048]{2,1,0:T(1,128)}, u32[]{:S(2)}) copy-start(s32[1,1,2048]{2,1,0:T(1,128)} %param.23) | copy-start | bytes 24580
  69.3 54.5 %all-to-all-start.1 = ((bf16[8,256,512]{1,2,0:T(8,128)(2,1)}), bf16[8,256,512]{1,2,0:T(8,128)(2,1)}, u32[]{:S(2)}, u32[]{:S(2)}) async-start(bf16[8,256,512]{1,2,0:T(8,128)(2,1)} %bitcast.37), calls=%async_computation.1 | async-start | bytes 4194304 | tf_op jit(solution)/shard_map/all_to_all | solution.py:73
  126.6 2.5 %copy-start.2 = (f32[2048,512]{1,0:T(8,128)S(1)}, f32[2048,512]{1,0:T(8,128)}, u32[]{:S(2)}) copy-start(f32[2048,512]{1,0:T(8,128)} %fusion.5) | copy-start | bytes 12582916
  126.7 2.5 %copy-start.7 = (f32[512]{0:T(512)S(1)}, f32[512]{0:T(512)}, u32[]{:S(2)}) copy-start(f32[512]{0:T(512)} %param.25) | copy-start | bytes 6148
  129.1 3.1 %copy-start.6 = (f32[512]{0:T(512)S(1)}, f32[512]{0:T(512)}, u32[]{:S(2)}) copy-start(f32[512]{0:T(512)} %param.27) | copy-start | bytes 6148
  133.6 1.6 %copy-start.3 = (bf16[1,1,2048,512]{2,3,1,0:T(8,128)(2,1)S(1)}, bf16[1,1,2048,512]{2,3,1,0:T(8,128)(2,1)}, u32[]{:S(2)}) copy-start(bf16[1,1,2048,512]{2,3,1,0:T(8,128)(2,1)} %copy.27) | copy-start | bytes 6291460
  133.6 1.6 %copy-start.8 = (f32[512]{0:T(512)S(1)}, f32[512]{0:T(512)}, u32[]{:S(2)}) copy-start(f32[512]{0:T(512)} %param.29) | copy-start | bytes 6148
  133.6 1.6 %copy-start.9 = (f32[512]{0:T(512)S(1)}, f32[512]{0:T(512)}, u32[]{:S(2)}) copy-start(f32[512]{0:T(512)} %param.28) | copy-start | bytes 6148
  135.2 8.9 %copy-start.10 = (f32[512]{0:T(512)S(1)}, f32[512]{0:T(512)}, u32[]{:S(2)}) copy-start(f32[512]{0:T(512)} %param.33) | copy-start | bytes 6148
  135.2 8.9 %copy-start.11 = (f32[512]{0:T(512)S(1)}, f32[512]{0:T(512)}, u32[]{:S(2)}) copy-start(f32[512]{0:T(512)} %param.31) | copy-start | bytes 6148
